TPU v7x, 32 devices: a whole 2x2x4 slice. The times are simulated.
32 devices in a mesh: row: 8 (over z, core), col: 4 (over y, x).
Axes of the slice: x: 2, y: 2, z: 4, core: 2. Of those that a mesh axis runs over, the one named last changes fastest.
Arguments:
- wrapped_phase: float32 [16384, 2048], P('row', 'col'), may hold values from -2.85 to 2.85, as said below
Outputs:
- unwrapped: float32 [16384, 2048], P('row', 'col')
Inputs may be any that keep to these rules, and one draw needn't show every extreme that they name: The difference of wrapped_phase between any two adjacent cells of the map lies 0.14 or more away from every odd multiple of pi.
All inputs are finite; a program needn't handle non-finite values.
Results may differ from a plain program's by a relative error of at most 0.0003.
Values sent between devices are 32-bit elements; how exact they have to be, the bound alone decides.
A program may use at most 128 MiB of HBM per device.

v0:
```python
import functools
import math

import jax
import jax.numpy as jnp
import numpy as np
from jax import lax
from jax.experimental import pallas as pl
from jax.experimental.pallas import tpu as pltpu
from jax.sharding import PartitionSpec as P

TILE = 256
FULL_TURN = 2.0 * math.pi
MESH = pl.DeviceIdType.MESH
LANES = 128


def wrap_turns(values):
    return values - jnp.round(values)


def cos32(angle):
    return np.cos(angle.astype(np.float64)).astype(np.float32)


def tables(length):
    f32 = np.float32
    order = np.arange(length, dtype=f32)
    angle = (f32(math.pi) * order)[:, None] * (f32(2) * order + f32(1))[None, :] / f32(2 * length)
    cosine = cos32(angle) * f32(math.sqrt(2.0 / length))
    cosine[0] = cosine[0] * f32(math.sqrt(0.5))
    wave = f32(2) * cos32(f32(math.pi) * order / f32(length))
    eigen = (wave[:, None] + wave[None, :]) - f32(4)
    eigen[0, 0] = -1
    inverse = 1.0 / eigen.astype(np.float64)
    inverse[0, 0] = 0
    c64 = cosine.astype(np.float64)
    weights = []
    for cell in (length - 1, 0):
        green = (c64[:, cell] * inverse[0]) @ c64
        step = green - np.append(green[1:], 0.0)
        step[-1] = 0
        weights.append(step / length)
    return cosine, inverse.astype(f32), np.stack(weights).astype(f32)


def split(values):
    high = values.astype(jnp.bfloat16)
    low = (values - high.astype(jnp.float32)).astype(jnp.bfloat16)
    return high, low


def dot(left, right):
    return jnp.dot(left, right, preferred_element_type=jnp.float32)


def stack3(high, low, axis):
    return jnp.concatenate([high, low, high], axis)


BLOCKS = TILE // LANES


def wide(ref, first, rows):
    return jnp.concatenate([ref[first + l, rows, :] for l in range(BLOCKS)], 1)


def put_wide(ref, first, rows, values):
    for l in range(values.shape[1] // LANES):
        ref[first + l, rows, :] = values[:, l * LANES : (l + 1) * LANES]


def in_blocks(table):
    return np.ascontiguousarray(
        table.reshape(table.shape[0], -1, LANES).transpose(1, 0, 2))


def sandwich(pairs, right, left):
    first, second = pl.ds(0, TILE), pl.ds(TILE, TILE)
    table = [wide(right, 0, first), wide(right, 0, first), wide(right, 0, second)]
    table = jnp.concatenate(table, 0)
    inner = [split(dot(stack3(high, low, 1), table)) for high, low in pairs]
    table = [wide(left, 0, first), wide(left, 0, first), wide(left, BLOCKS, first)]
    table = jnp.concatenate(table, 1)
    return [dot(table, stack3(high, low, 0)) for high, low in inner]


def group_size(bands, most):
    return next(g for g in range(most, 0, -1) if bands % g == 0)


def band_rows(i):
    return pl.ds(pl.multiple_of(i * TILE, TILE), TILE)


def band_copy(src, dst, sem, i):
    rows = band_rows(i)
    view = lambda ref: ref.at[rows, :] if len(ref.shape) == 2 else ref.at[:, rows, :]
    return pltpu.make_async_copy(view(src), view(dst), sem.at[i])


def finish_kernel(
    high_hbm, low_hbm, off_ref, left, right, out_hbm, high_s, low_s, out_s, high_sem, low_sem, out_sem
):
    height, width = out_s.shape
    bands, tiles = height // TILE, width // TILE
    for i in range(bands):
        band_copy(high_hbm, high_s, high_sem, i).start()
        band_copy(low_hbm, low_s, low_sem, i).start()

    group = group_size(bands, 2)

    def step(j, carry):
        some = [j * group + k for k in range(group)]
        for i in some:
            band_copy(high_hbm, high_s, high_sem, i).wait()
            band_copy(low_hbm, low_s, low_sem, i).wait()
        places = [(i, t) for i in some for t in range(tiles)]
        pairs = [
            (wide(high_s, t * BLOCKS, band_rows(i)), wide(low_s, t * BLOCKS, band_rows(i)))
            for i, t in places
        ]
        for (i, t), solved in zip(places, sandwich(pairs, right, left)):
            cols = slice(t * TILE, (t + 1) * TILE)
            out_s[band_rows(i), cols] = solved + off_ref[pl.ds(i, 1), cols]
        for i in some:
            band_copy(out_s, out_hbm, out_sem, i).start()
        return carry

    lax.fori_loop(0, bands // group, step, 0)
    for i in range(bands):
        band_copy(out_s, out_hbm, out_sem, i).wait()


def lane_sum(values):
    return jnp.sum(values, axis=1, keepdims=True)


def running(values):
    n = values.shape[0]
    row = lax.broadcasted_iota(jnp.int32, values.shape, 0)
    total = jnp.zeros_like(values)
    for k in range(n - 1):
        total = total + jnp.where(row > k, values[k : k + 1], 0.0)
    return total


CHUNK = 32


def slope_band(x_s, w_ref, i, bands, dh_s, dl_s, sum_s, sum_d, first_s, last_s):
    width = x_s.shape[1]
    base = pl.multiple_of(i * TILE, TILE)
    shape = (CHUNK, width)
    row_id = lax.broadcasted_iota(jnp.int32, shape, 0)
    tile_end = lax.broadcasted_iota(jnp.int32, shape, 1) % TILE == TILE - 1
    fold = lambda v: jnp.sum(v.reshape(CHUNK // 8, 8, v.shape[1]), axis=0)
    acc = jnp.zeros((8, width), jnp.float32)
    acc_last = jnp.zeros((8, TILE), jnp.float32)
    acc_first = jnp.zeros((8, TILE), jnp.float32)
    before = jnp.zeros((1, width), jnp.float32)
    for k in range(TILE // CHUNK):
        rows = pl.ds(base + k * CHUNK, CHUNK)
        x = x_s[rows, :] * (1.0 / FULL_TURN)
        below = pltpu.roll(x, CHUNK - 1, 0)
        if k < TILE // CHUNK - 1:
            below = jnp.where(row_id == CHUNK - 1, x_s[pl.ds(base + (k + 1) * CHUNK, 1), :] * (1.0 / FULL_TURN), below)
        down = wrap_turns(below - x)
        if k == TILE // CHUNK - 1:
            down = jnp.where(row_id == CHUNK - 1, 0.0, down)
        across = wrap_turns(pltpu.roll(x, width - 1, 1) - x)
        acc = acc + fold(across)
        weight = w_ref[k * CHUNK : (k + 1) * CHUNK, 2 * TILE : 2 * TILE + 2]
        acc_last = acc_last + fold(down[:, :TILE] * weight[:, 0:1])
        acc_first = acc_first + fold(down[:, :TILE] * weight[:, 1:2])
        across = jnp.where(tile_end, 0.0, across)
        above = jnp.where(row_id == 0, before, pltpu.roll(down, 1, 0))
        before = down[CHUNK - 1 : CHUNK, :]
        high, low = split(down - above + across - pltpu.roll(across, 1, 1))
        put_wide(dh_s, 0, rows, high)
        put_wide(dl_s, 0, rows, low)
    sum_s[pl.ds(i, 1), :] = jnp.sum(acc, axis=0, keepdims=True)
    sum_d[pl.ds(i, 1), :] = jnp.sum(acc_last, axis=0, keepdims=True)
    sum_d[pl.ds(bands + i, 1), :] = jnp.sum(acc_first, axis=0, keepdims=True)
    first_s[pl.ds(i, 1), :] = x_s[pl.ds(base, 1), 0:TILE]
    last_s[pl.ds(i, 1), :] = x_s[pl.ds(base + TILE - 1, 1), 0:TILE]


def chain_kernel(
    n_row, n_col, x_hbm, w_ref, left, right, inv_ref, high_hbm, low_hbm, off_ref,
    x_s, dh_s, dl_s, sh_s, sl_s,
    col_out, col_in, top_out, top_in, sum_s, sum_d, first_s, last_s,
    down_out, down_in, row_out, row_in,
    edge_send, edge_recv, down_send, down_recv, row_send, row_recv,
    x_sem, high_sem, low_sem,
):
    r, c = lax.axis_index("row"), lax.axis_index("col")
    height, width = x_s.shape
    bands, tiles = height // TILE, width // TILE
    for i in range(bands):
        band_copy(x_hbm, x_s, x_sem, i).start()

    barrier = pltpu.get_barrier_semaphore()
    for k in range(1, n_row):
        pl.semaphore_signal(barrier, inc=1, device_id=(lax.rem(r + k, n_row), c), device_id_type=MESH)
    for k in range(1, n_col):
        pl.semaphore_signal(barrier, inc=1, device_id=(r, lax.rem(c + k, n_col)), device_id_type=MESH)

    def take_columns(i, carry):
        band_copy(x_hbm, x_s, x_sem, i).wait()
        rows = band_rows(i)
        col_out[pl.ds(i, 1), :] = jnp.transpose(x_s[rows, 0:LANES])[0:1, :]
        ends = jnp.transpose(x_s[rows, width - LANES : width])
        last_s[pl.ds(bands + i, 1), :] = ends[LANES - 1 : LANES, :]
        return carry

    lax.fori_loop(0, bands, take_columns, 0)
    top_out[...] = jnp.broadcast_to(x_s[0:1, 0:TILE], top_out.shape)

    pl.semaphore_wait(barrier, n_row + n_col - 2)
    edge_col = pltpu.make_async_remote_copy(
        src_ref=col_out, dst_ref=col_in, send_sem=edge_send.at[0], recv_sem=edge_recv.at[0],
        device_id=(r, lax.rem(c + n_col - 1, n_col)), device_id_type=MESH)
    edge_top = pltpu.make_async_remote_copy(
        src_ref=top_out, dst_ref=top_in, send_sem=edge_send.at[1], recv_sem=edge_recv.at[1],
        device_id=(lax.rem(r + n_row - 1, n_row), c), device_id_type=MESH)
    edge_col.start()
    edge_top.start()

    def slope_step(i, carry):
        slope_band(x_s, w_ref, i, bands, dh_s, dl_s, sum_s, sum_d, first_s, last_s)
        return carry

    lax.fori_loop(0, bands, slope_step, 0)

    group = group_size(bands // 2, 4)

    def spectrum_step(j, carry):
        some = [j * group + k for k in range(group)]
        places = [(i, t) for i in some for t in range(tiles)]
        pairs = [
            (wide(dh_s, t * BLOCKS, band_rows(i)), wide(dl_s, t * BLOCKS, band_rows(i)))
            for i, t in places
        ]
        for (i, t), spectrum in zip(places, sandwich(pairs, right, left)):
            high, low = split(spectrum * inv_ref[...])
            put_wide(sh_s, t * BLOCKS, band_rows(i), high)
            put_wide(sl_s, t * BLOCKS, band_rows(i), low)
        for i in some:
            band_copy(sh_s, high_hbm, high_sem, i).start()
            band_copy(sl_s, low_hbm, low_sem, i).start()
        return carry

    scale = FULL_TURN / TILE
    down_last = lane_sum(sum_d[0:bands, :])
    down_first = lane_sum(sum_d[bands : 2 * bands, :])
    edge_top.wait()
    edge_col.wait()
    below = jnp.concatenate([first_s[1:bands, :], top_in[0:1, :]], 0)
    border = lane_sum(wrap_turns((below - last_s[0:bands, :]) * (1.0 / FULL_TURN))) * scale
    band_id = lax.broadcasted_iota(jnp.int32, (bands, 1), 0)
    next_first = jnp.concatenate([down_first[1:bands], down_first[0:1]], 0)
    jump = down_last + border - next_first
    jump_total = jnp.sum(jump, axis=0, keepdims=True)
    starts = running(jump)
    lane = lax.broadcasted_iota(jnp.int32, (8, LANES), 1)
    down_first0 = down_first[0:1]
    down_out[...] = jnp.where(lane == 0, jump_total, jnp.where(lane == 1, down_first0, 0.0))
    copies = []
    for k in range(1, n_row):
        copies.append(pltpu.make_async_remote_copy(
            src_ref=down_out, dst_ref=down_in.at[k - 1],
            send_sem=down_send.at[k - 1], recv_sem=down_recv.at[k - 1],
            device_id=(lax.rem(r + k, n_row), c), device_id_type=MESH))
    for copy in copies:
        copy.start()

    sums = sum_s[...]
    last_w, first_w = w_ref[0:1, 0:TILE], w_ref[0:1, TILE : 2 * TILE]
    lasts = [lane_sum(sums[:, t * TILE : (t + 1) * TILE] * last_w) for t in range(tiles)]
    firsts = [lane_sum(sums[:, t * TILE : (t + 1) * TILE] * first_w) for t in range(tiles)]
    along = [jnp.zeros((bands, 1), jnp.float32)]
    for t in range(tiles - 1):
        end = (t + 1) * TILE
        along.append(along[-1] + lasts[t] + sums[:, end - 1 : end] * scale - firsts[t + 1])
    edge = lane_sum(wrap_turns((col_in[...] - last_s[bands : 2 * bands, :]) * (1.0 / FULL_TURN))) * scale
    row_total = along[-1] + lasts[-1] + edge - firsts[0]

    half = bands // 2 // group
    lax.fori_loop(0, half, spectrum_step, 0)
    for copy in copies:
        copy.wait()
    above = jnp.zeros((1, 1), jnp.float32)
    origin = jnp.where(r == 0, down_first0, 0.0)
    for k in range(1, n_row):
        got = down_in[k - 1]
        above = above + jnp.where(k <= r, got[0:1, 0:1], 0.0)
        origin = origin + jnp.where(k == r, got[0:1, 1:2], 0.0)
    starts = starts + above + origin - down_first0

    lane = lax.broadcasted_iota(jnp.int32, (bands, LANES), 1)
    row_out[...] = jnp.where(
        lane == 0, row_total, jnp.where(lane == 1, starts + firsts[0], 0.0))
    copies = []
    for k in range(1, n_col):
        copies.append(pltpu.make_async_remote_copy(
            src_ref=row_out, dst_ref=row_in.at[k - 1],
            send_sem=row_send.at[k - 1], recv_sem=row_recv.at[k - 1],
            device_id=(r, lax.rem(c + k, n_col)), device_id_type=MESH))
    for copy in copies:
        copy.start()
    lax.fori_loop(half, bands // group, spectrum_step, 0)
    for copy in copies:
        copy.wait()
    offset = jnp.where(c == 0, starts + firsts[0], 0.0) - firsts[0]
    for k in range(1, n_col):
        got = row_in[k - 1]
        offset = offset + jnp.where(k <= c, got[:, 0:1], 0.0)
        offset = offset + jnp.where(k == c, got[:, 1:2], 0.0)
    for t in range(tiles):
        off_ref[:, t * TILE : (t + 1) * TILE] = jnp.broadcast_to(offset + along[t], (bands, TILE))
    for i in range(bands):
        band_copy(sh_s, high_hbm, high_sem, i).wait()
        band_copy(sl_s, low_hbm, low_sem, i).wait()


def per_device(n_row, n_col, x):
    height, width = x.shape
    bands = height // TILE
    blocks = (width // LANES, height, LANES)
    cosine, inverse, weights = tables(TILE)
    high = cosine.astype(jnp.bfloat16)
    low = (cosine - high.astype(np.float32)).astype(jnp.bfloat16)
    beside = in_blocks(np.concatenate([high, low], 1))
    over = in_blocks(np.concatenate([high, low], 0))
    beside_t = in_blocks(np.concatenate([high.T, low.T], 1))
    over_t = in_blocks(np.concatenate([high.T, low.T], 0))
    w = np.zeros((TILE, 2 * TILE + LANES), np.float32)
    weights = weights * np.float32(FULL_TURN)
    w[:, 0:TILE] = weights[0]
    w[:, TILE : 2 * TILE] = weights[1]
    w[:, 2 * TILE] = weights[0]
    w[:, 2 * TILE + 1] = weights[1]

    vmem = pl.BlockSpec(memory_space=pltpu.VMEM)
    anywhere = pl.BlockSpec(memory_space=pl.ANY)
    f32, bf16 = jnp.float32, jnp.bfloat16
    high_s, low_s, offsets = pl.pallas_call(
        functools.partial(chain_kernel, n_row, n_col),
        out_shape=[
            jax.ShapeDtypeStruct(blocks, bf16),
            jax.ShapeDtypeStruct(blocks, bf16),
            jax.ShapeDtypeStruct((bands, width), f32),
        ],
        in_specs=[anywhere] + [vmem] * 4,
        out_specs=[anywhere, anywhere, vmem],
        scratch_shapes=[
            pltpu.VMEM((height, width), f32),
            pltpu.VMEM(blocks, bf16),
            pltpu.VMEM(blocks, bf16),
            pltpu.VMEM(blocks, bf16),
            pltpu.VMEM(blocks, bf16),
            pltpu.VMEM((bands, TILE), f32),
            pltpu.VMEM((bands, TILE), f32),
            pltpu.VMEM((8, TILE), f32),
            pltpu.VMEM((8, TILE), f32),
            pltpu.VMEM((bands, width), f32),
            pltpu.VMEM((2 * bands, TILE), f32),
            pltpu.VMEM((bands, TILE), f32),
            pltpu.VMEM((2 * bands, TILE), f32),
            pltpu.VMEM((8, LANES), f32),
            pltpu.VMEM((n_row - 1, 8, LANES), f32),
            pltpu.VMEM((bands, LANES), f32),
            pltpu.VMEM((n_col - 1, bands, LANES), f32),
            pltpu.SemaphoreType.DMA((2,)),
            pltpu.SemaphoreType.DMA((2,)),
            pltpu.SemaphoreType.DMA((n_row - 1,)),
            pltpu.SemaphoreType.DMA((n_row - 1,)),
            pltpu.SemaphoreType.DMA((n_col - 1,)),
            pltpu.SemaphoreType.DMA((n_col - 1,)),
            pltpu.SemaphoreType.DMA((bands,)),
            pltpu.SemaphoreType.DMA((bands,)),
            pltpu.SemaphoreType.DMA((bands,)),
        ],
        compiler_params=pltpu.CompilerParams(collective_id=0, has_side_effects=True),
        name="chain",
    )(x, jnp.asarray(w), jnp.asarray(beside), jnp.asarray(over_t), jnp.asarray(inverse * np.float32(FULL_TURN)))

    return pl.pallas_call(
        finish_kernel,
        out_shape=jax.ShapeDtypeStruct(x.shape, f32),
        in_specs=[anywhere, anywhere, vmem, vmem, vmem],
        out_specs=anywhere,
        scratch_shapes=[
            pltpu.VMEM(blocks, bf16),
            pltpu.VMEM(blocks, bf16),
            pltpu.VMEM((height, width), f32),
            pltpu.SemaphoreType.DMA((bands,)),
            pltpu.SemaphoreType.DMA((bands,)),
            pltpu.SemaphoreType.DMA((bands,)),
        ],
        name="finish",
    )(high_s, low_s, offsets, jnp.asarray(beside_t), jnp.asarray(over))


def solution(mesh):
    n_row, n_col = mesh.shape["row"], mesh.shape["col"]
    return jax.shard_map(
        functools.partial(per_device, n_row, n_col), mesh=mesh,
        in_specs=(P("row", "col"),), out_specs=P("row", "col"), check_vma=False,
    )
```

profile of v0, /device:TPU:0, one launch (start us, length us, event | category | flops | bytes accessed | tf_op | source)
XLA Modules:
  0.0 28.8 jit_solution(12583288037592426306)
XLA Ops:
  0.0 21.5 %chain.1 = (bf16[4,2048,128]{2,1,0:T(8,128)(2,1)}, bf16[4,2048,128]{2,1,0:T(8,128)(2,1)}, f32[8,512]{1,0:T(8,128)}) custom-call(f32[2048,512]{1,0:T(8,128)} %x_hbm.1, f32[256,640]{1,0:T(8,128)} %constant.12.clone.w_ref, bf16[4,256,128]{2,1,0:T(8,128)(2,1)} %constant.13.clone.left, bf16[2,512,128]{2,1,0:T(8,128)(2,1)} %constant.14.clone.right, ...), custom_call_target="tpu_custom_call" | custom-call | tf_op jit(solution)/shard_map/chain/pallas_call | solution.py:348
  21.5 7.4 %finish.1 = f32[2048,512]{1,0:T(8,128)} custom-call(bf16[4,2048,128]{2,1,0:T(8,128)(2,1)} %get-tuple-element.8.high_hbm, bf16[4,2048,128]{2,1,0:T(8,128)(2,1)} %get-tuple-element.9.low_hbm, f32[8,512]{1,0:T(8,128)} %get-tuple-element.10.off_ref, bf16[4,256,128]{2,1,0:T(8,128)(2,1)} %constant.16.clone.left, bf16[2,512,128]{2,1,0:T(8,128)(2,1)} %constant.17.clone.right), custom_call_target="tpu_custom_call" | custom-call | tf_op jit(solution)/shard_map/finish/pallas_call | solution.py:389
where the time goes:
time: 29 us; the launch traced here: 28.8 us
  Pallas kernels  28.8 us (99%)
    pallas_call x1, Pallas kernels, per_device(): pl.pallas_call(functools.partial(chain_kernel, n_row, n_col), out_shape=[...  21.5 us
    pallas_call x1, Pallas kernels, per_device(): pl.pallas_call(finish_kernel, out_shape=jax.ShapeDtypeStruct(x.shape, f32...  7.36 us

commit v1 on v0

v1 whole, which is shorter than its diff:
```python
import functools
import math

import jax
import jax.numpy as jnp
import numpy as np
from jax import lax
from jax.experimental import pallas as pl
from jax.experimental.pallas import tpu as pltpu
from jax.sharding import PartitionSpec as P

TILE = 256
FULL_TURN = 2.0 * math.pi
MESH = pl.DeviceIdType.MESH
LANES = 128


def wrap_turns(values):
    return values - jnp.round(values)


def cos32(angle):
    return np.cos(angle.astype(np.float64)).astype(np.float32)


def tables(length):
    f32 = np.float32
    order = np.arange(length, dtype=f32)
    angle = (f32(math.pi) * order)[:, None] * (f32(2) * order + f32(1))[None, :] / f32(2 * length)
    cosine = cos32(angle) * f32(math.sqrt(2.0 / length))
    cosine[0] = cosine[0] * f32(math.sqrt(0.5))
    wave = f32(2) * cos32(f32(math.pi) * order / f32(length))
    eigen = (wave[:, None] + wave[None, :]) - f32(4)
    eigen[0, 0] = -1
    inverse = 1.0 / eigen.astype(np.float64)
    inverse[0, 0] = 0
    c64 = cosine.astype(np.float64)
    weights = []
    for cell in (length - 1, 0):
        green = (c64[:, cell] * inverse[0]) @ c64
        step = green - np.append(green[1:], 0.0)
        step[-1] = 0
        weights.append(step / length)
    return cosine, inverse.astype(f32), np.stack(weights).astype(f32)


def split(values):
    high = values.astype(jnp.bfloat16)
    low = (values - high.astype(jnp.float32)).astype(jnp.bfloat16)
    return high, low


def dot(left, right):
    return jnp.dot(left, right, preferred_element_type=jnp.float32)


def stack3(high, low, axis):
    return jnp.concatenate([high, low, high], axis)


BLOCKS = TILE // LANES


def wide(ref, first, rows):
    return jnp.concatenate([ref[first + l, rows, :] for l in range(BLOCKS)], 1)


def put_wide(ref, first, rows, values):
    for l in range(values.shape[1] // LANES):
        ref[first + l, rows, :] = values[:, l * LANES : (l + 1) * LANES]


def in_blocks(table):
    return np.ascontiguousarray(
        table.reshape(table.shape[0], -1, LANES).transpose(1, 0, 2))


def sandwich(pairs, right, left):
    first, second = pl.ds(0, TILE), pl.ds(TILE, TILE)
    table = [wide(right, 0, first), wide(right, 0, first), wide(right, 0, second)]
    table = jnp.concatenate(table, 0)
    inner = [split(dot(stack3(high, low, 1), table)) for high, low in pairs]
    table = [wide(left, 0, first), wide(left, 0, first), wide(left, BLOCKS, first)]
    table = jnp.concatenate(table, 1)
    return [dot(table, stack3(high, low, 0)) for high, low in inner]


def group_size(bands, most):
    return next(g for g in range(most, 0, -1) if bands % g == 0)


def band_rows(i):
    return pl.ds(pl.multiple_of(i * TILE, TILE), TILE)


def band_copy(src, dst, sem, i):
    rows = band_rows(i)
    view = lambda ref: ref.at[rows, :] if len(ref.shape) == 2 else ref.at[:, rows, :]
    return pltpu.make_async_copy(view(src), view(dst), sem.at[i])


def lane_sum(values):
    return jnp.sum(values, axis=1, keepdims=True)


def running(values):
    n = values.shape[0]
    row = lax.broadcasted_iota(jnp.int32, values.shape, 0)
    total = jnp.zeros_like(values)
    for k in range(n - 1):
        total = total + jnp.where(row > k, values[k : k + 1], 0.0)
    return total


CHUNK = 32


def slope_band(x_s, w_ref, i, bands, dh_s, dl_s, sum_s, sum_d, first_s, last_s):
    width = x_s.shape[1]
    base = pl.multiple_of(i * TILE, TILE)
    shape = (CHUNK, width)
    row_id = lax.broadcasted_iota(jnp.int32, shape, 0)
    tile_end = lax.broadcasted_iota(jnp.int32, shape, 1) % TILE == TILE - 1
    fold = lambda v: jnp.sum(v.reshape(CHUNK // 8, 8, v.shape[1]), axis=0)
    acc = jnp.zeros((8, width), jnp.float32)
    acc_last = jnp.zeros((8, TILE), jnp.float32)
    acc_first = jnp.zeros((8, TILE), jnp.float32)
    before = jnp.zeros((1, width), jnp.float32)
    for k in range(TILE // CHUNK):
        rows = pl.ds(base + k * CHUNK, CHUNK)
        x = x_s[rows, :] * (1.0 / FULL_TURN)
        below = pltpu.roll(x, CHUNK - 1, 0)
        if k < TILE // CHUNK - 1:
            below = jnp.where(row_id == CHUNK - 1, x_s[pl.ds(base + (k + 1) * CHUNK, 1), :] * (1.0 / FULL_TURN), below)
        down = wrap_turns(below - x)
        if k == TILE // CHUNK - 1:
            down = jnp.where(row_id == CHUNK - 1, 0.0, down)
        across = wrap_turns(pltpu.roll(x, width - 1, 1) - x)
        acc = acc + fold(across)
        weight = w_ref[k * CHUNK : (k + 1) * CHUNK, 2 * TILE : 2 * TILE + 2]
        acc_last = acc_last + fold(down[:, :TILE] * weight[:, 0:1])
        acc_first = acc_first + fold(down[:, :TILE] * weight[:, 1:2])
        across = jnp.where(tile_end, 0.0, across)
        above = jnp.where(row_id == 0, before, pltpu.roll(down, 1, 0))
        before = down[CHUNK - 1 : CHUNK, :]
        high, low = split(down - above + across - pltpu.roll(across, 1, 1))
        put_wide(dh_s, 0, rows, high)
        put_wide(dl_s, 0, rows, low)
    sum_s[pl.ds(i, 1), :] = jnp.sum(acc, axis=0, keepdims=True)
    sum_d[pl.ds(i, 1), :] = jnp.sum(acc_last, axis=0, keepdims=True)
    sum_d[pl.ds(bands + i, 1), :] = jnp.sum(acc_first, axis=0, keepdims=True)
    first_s[pl.ds(i, 1), :] = x_s[pl.ds(base, 1), 0:TILE]
    last_s[pl.ds(i, 1), :] = x_s[pl.ds(base + TILE - 1, 1), 0:TILE]


def compact(x_s, column):
    height = x_s.shape[0]
    lane = lax.broadcasted_iota(jnp.int32, (8, LANES), 1)
    block = column // LANES * LANES
    rows = []
    for g in range(height // (8 * LANES)):
        acc = jnp.zeros((8, LANES), jnp.float32)
        for k in range(LANES):
            cells = x_s[pl.ds((g * LANES + k) * 8, 8), block : block + LANES]
            acc = jnp.where(lane == k, pltpu.roll(cells, (k - column) % LANES, 1), acc)
        rows.append(acc)
    return jnp.concatenate(rows, 0)


def band_sums(values, bands):
    span = TILE // 8
    row = lax.broadcasted_iota(jnp.int32, (bands, LANES), 0)
    lane = lax.broadcasted_iota(jnp.int32, (bands, LANES), 1)
    per = LANES // span
    sums = jnp.sum(values.reshape(-1, 8, LANES), axis=1)
    picked = jnp.concatenate(
        [jnp.broadcast_to(sums[i // per : i // per + 1], (1, LANES)) for i in range(bands)], 0)
    return lane_sum(jnp.where(lane // span == row % per, picked, 0.0))


def chain_kernel(
    n_row, n_col, x_hbm, w_hbm, left_hbm, right_hbm, left_t_hbm, right_t_hbm, inv_hbm, u_ref, off_ref,
    x_s, w_ref, left, right, left_t, right_t, inv_ref, dh_s, dl_s, sh_s, sl_s,
    col_out, col_in, top_out, top_in, sum_s, sum_d, first_s, last_s,
    down_out, down_in, row_out, row_in,
    edge_send, edge_recv, down_send, down_recv, row_send, row_recv,
    x_sem, table_sem,
):
    r, c = lax.axis_index("row"), lax.axis_index("col")
    height, width = x_s.shape
    bands, tiles = height // TILE, width // TILE
    band_copy(x_hbm, x_s, x_sem, 0).start()
    tables = [(w_hbm, w_ref), (right_hbm, right), (left_hbm, left), (inv_hbm, inv_ref),
              (right_t_hbm, right_t), (left_t_hbm, left_t)]
    tables = [pltpu.make_async_copy(a, b, table_sem.at[k]) for k, (a, b) in enumerate(tables)]
    tables[0].start()
    for i in range(1, bands):
        band_copy(x_hbm, x_s, x_sem, i).start()
    for copy in tables[1:]:
        copy.start()

    barrier = pltpu.get_barrier_semaphore()

    def greet(row, col):
        pl.semaphore_signal(barrier, inc=1, device_id=(row, col), device_id_type=MESH)

    def greet_above(k, carry):
        greet(k, 0)
        return carry

    def greet_left(k, carry):
        greet(r, k)
        return carry

    lax.fori_loop(0, r, greet_above, 0)
    lax.fori_loop(0, c, greet_left, 0)
    is_first = c == 0
    has_right = c < n_col - 1
    has_below = r < n_row - 1
    pl.when(has_right)(lambda: greet(r, c + 1))
    pl.when(jnp.logical_and(is_first, has_below))(lambda: greet(r + 1, 0))

    def slopes(i):
        slope_band(x_s, w_ref, i, bands, dh_s, dl_s, sum_s, sum_d, first_s, last_s)

    def forward(bands_):
        places = [(i, t) for i in bands_ for t in range(tiles)]
        pairs = [
            (wide(dh_s, t * BLOCKS, band_rows(i)), wide(dl_s, t * BLOCKS, band_rows(i)))
            for i, t in places
        ]
        for (i, t), spectrum in zip(places, sandwich(pairs, right, left)):
            high, low = split(spectrum * inv_ref[...])
            put_wide(sh_s, t * BLOCKS, band_rows(i), high)
            put_wide(sl_s, t * BLOCKS, band_rows(i), low)

    def backward(bands_):
        places = [(i, t) for i in bands_ for t in range(tiles)]
        pairs = [
            (wide(sh_s, t * BLOCKS, band_rows(i)), wide(sl_s, t * BLOCKS, band_rows(i)))
            for i, t in places
        ]
        for (i, t), solved in zip(places, sandwich(pairs, right_t, left_t)):
            u_ref[band_rows(i), t * TILE : (t + 1) * TILE] = solved

    band_copy(x_hbm, x_s, x_sem, 0).wait()
    tables[0].wait()
    slopes(0)
    for i in range(1, bands):
        band_copy(x_hbm, x_s, x_sem, i).wait()
    for copy in tables[1:]:
        copy.wait()
    col_out[...] = compact(x_s, 0)
    top_out[...] = jnp.broadcast_to(x_s[0:1, 0:TILE], top_out.shape)

    peers = (n_col - 1 - c) + jnp.where(is_first, 0, 1)
    peers = peers + jnp.where(is_first, (n_row - 1 - r) * n_col + jnp.where(r > 0, 1, 0), 0)
    pl.semaphore_wait(barrier, peers)
    edge_col = pltpu.make_async_remote_copy(
        src_ref=col_out, dst_ref=col_in, send_sem=edge_send.at[0], recv_sem=edge_recv.at[0],
        device_id=(r, jnp.maximum(c - 1, 0)), device_id_type=MESH)
    edge_top = pltpu.make_async_remote_copy(
        src_ref=top_out, dst_ref=top_in, send_sem=edge_send.at[1], recv_sem=edge_recv.at[1],
        device_id=(jnp.maximum(r - 1, 0), c), device_id_type=MESH)
    send_top = jnp.logical_and(is_first, r > 0)
    pl.when(jnp.logical_not(is_first))(lambda: edge_col.start())
    pl.when(send_top)(lambda: edge_top.start())

    last_col = compact(x_s, width - 1)
    for i in range(1, bands):
        slopes(i)
        if i % 2 == 1:
            forward([i - 1, i])

    scale = FULL_TURN / TILE
    sums = sum_s[...]
    last_w, first_w = w_ref[0:1, 0:TILE], w_ref[0:1, TILE : 2 * TILE]
    lasts = [lane_sum(sums[:, t * TILE : (t + 1) * TILE] * last_w) for t in range(tiles)]
    firsts = [lane_sum(sums[:, t * TILE : (t + 1) * TILE] * first_w) for t in range(tiles)]
    along = [jnp.zeros((bands, 1), jnp.float32)]
    for t in range(tiles - 1):
        end = (t + 1) * TILE
        along.append(along[-1] + lasts[t] + sums[:, end - 1 : end] * scale - firsts[t + 1])
    down_last = lane_sum(sum_d[0:bands, :])
    down_first = lane_sum(sum_d[bands : 2 * bands, :])
    down_first0 = down_first[0:1]

    down_copy = lambda row, col: pltpu.make_async_remote_copy(
        src_ref=down_out, dst_ref=down_in.at[r], send_sem=down_send, recv_sem=down_recv.at[r],
        device_id=(row, col), device_id_type=MESH)
    row_copy = lambda k: pltpu.make_async_remote_copy(
        src_ref=row_out, dst_ref=row_in.at[c], send_sem=row_send, recv_sem=row_recv.at[c],
        device_id=(r, k), device_id_type=MESH)

    pl.when(jnp.logical_and(is_first, has_below))(lambda: edge_top.wait_recv())
    below = jnp.concatenate([first_s[1:bands, :], top_in[0:1, :]], 0)
    border = lane_sum(wrap_turns((below - last_s[0:bands, :]) * (1.0 / FULL_TURN))) * scale
    next_first = jnp.concatenate([down_first[1:bands], down_first[0:1]], 0)
    jump = down_last + border - next_first
    jump_total = jnp.sum(jump, axis=0, keepdims=True)
    starts = running(jump) - jnp.where(r > 0, down_first0, 0.0)
    lane = lax.broadcasted_iota(jnp.int32, (8, LANES), 1)
    down_out[...] = jnp.where(lane == 0, jump_total, jnp.where(lane == 1, down_first0, 0.0))
    n_down = jnp.where(is_first, (n_row - 1 - r) * n_col, 0)

    def send_down(k, carry):
        down_copy(r + 1 + k // n_col, k % n_col).start()
        return carry

    lax.fori_loop(0, n_down, send_down, 0)

    pl.when(has_right)(lambda: edge_col.wait_recv())
    edge = wrap_turns((col_in[...] - last_col) * (1.0 / FULL_TURN))
    row_total = along[-1] + lasts[-1] + band_sums(edge, bands) * scale - firsts[0]
    lane = lax.broadcasted_iota(jnp.int32, (bands, LANES), 1)
    row_out[...] = jnp.where(
        lane == 0, row_total, jnp.where(lane == 1, starts + firsts[0], 0.0))

    def send_row(k, carry):
        row_copy(k).start()
        return carry

    lax.fori_loop(c + 1, n_col, send_row, 0)

    for j in range(bands // 4):
        backward([4 * j + k for k in range(4)])

    pl.when(jnp.logical_not(is_first))(lambda: edge_col.wait_send())
    pl.when(send_top)(lambda: edge_top.wait_send())

    def sent_down(k, carry):
        down_copy(r + 1 + k // n_col, k % n_col).wait_send()
        return carry

    lax.fori_loop(0, n_down, sent_down, 0)

    def sent_row(k, carry):
        row_copy(k).wait_send()
        return carry

    lax.fori_loop(c + 1, n_col, sent_row, 0)

    above = jnp.zeros((1, 1), jnp.float32)
    for k in range(n_row - 1):
        pl.when(k < r)(lambda: pltpu.make_async_remote_copy(
            src_ref=down_out, dst_ref=down_in.at[k], send_sem=down_send, recv_sem=down_recv.at[k],
            device_id=(r, c), device_id_type=MESH).wait_recv())
        above = above + jnp.where(k < r, down_in[k, 0:1, 0:1], 0.0)
    above = above + jnp.where(r > 0, down_in[0, 0:1, 1:2], 0.0)
    offset = jnp.where(is_first, starts, -firsts[0]) + above
    for k in range(n_col - 1):
        pl.when(k < c)(lambda: pltpu.make_async_remote_copy(
            src_ref=row_out, dst_ref=row_in.at[k], send_sem=row_send, recv_sem=row_recv.at[k],
            device_id=(r, c), device_id_type=MESH).wait_recv())
        offset = offset + jnp.where(k < c, row_in[k, :, 0:1], 0.0)
    offset = offset + jnp.where(c > 0, row_in[0, :, 1:2], 0.0)
    for t in range(tiles):
        off_ref[:, t * TILE : (t + 1) * TILE] = jnp.broadcast_to(offset + along[t], (bands, TILE))


def finish_kernel(u_ref, off_ref, out_hbm, out_s, out_sem):
    height, width = out_s.shape
    bands = height // TILE
    for i in range(bands):
        rows = band_rows(i)
        out_s[rows, :] = u_ref[rows, :] + off_ref[i : i + 1, :]
        band_copy(out_s, out_hbm, out_sem, i).start()
    for i in range(bands):
        band_copy(out_s, out_hbm, out_sem, i).wait()


def per_device(n_row, n_col, x):
    height, width = x.shape
    bands = height // TILE
    blocks = (width // LANES, height, LANES)
    cosine, inverse, weights = tables(TILE)
    high = cosine.astype(jnp.bfloat16)
    low = (cosine - high.astype(np.float32)).astype(jnp.bfloat16)
    beside = in_blocks(np.concatenate([high, low], 1))
    over = in_blocks(np.concatenate([high, low], 0))
    beside_t = in_blocks(np.concatenate([high.T, low.T], 1))
    over_t = in_blocks(np.concatenate([high.T, low.T], 0))
    w = np.zeros((TILE, 2 * TILE + LANES), np.float32)
    weights = weights * np.float32(FULL_TURN)
    w[:, 0:TILE] = weights[0]
    w[:, TILE : 2 * TILE] = weights[1]
    w[:, 2 * TILE] = weights[0]
    w[:, 2 * TILE + 1] = weights[1]

    vmem = pl.BlockSpec(memory_space=pltpu.VMEM)
    hbm = pl.BlockSpec(memory_space=pltpu.HBM)
    f32, bf16 = jnp.float32, jnp.bfloat16
    consts = [w, beside, over_t, beside_t, over, inverse * np.float32(FULL_TURN)]
    u, offsets = pl.pallas_call(
        functools.partial(chain_kernel, n_row, n_col),
        out_shape=[pltpu.VMEM(x.shape, f32), pltpu.VMEM((bands, width), f32)],
        in_specs=[hbm] * 7,
        out_specs=[vmem, vmem],
        scratch_shapes=[pltpu.VMEM((height, width), f32)]
        + [pltpu.VMEM(t.shape, t.dtype) for t in consts]
        + [
            pltpu.VMEM(blocks, bf16),
            pltpu.VMEM(blocks, bf16),
            pltpu.VMEM(blocks, bf16),
            pltpu.VMEM(blocks, bf16),
            pltpu.VMEM((height // LANES, LANES), f32),
            pltpu.VMEM((height // LANES, LANES), f32),
            pltpu.VMEM((8, TILE), f32),
            pltpu.VMEM((8, TILE), f32),
            pltpu.VMEM((bands, width), f32),
            pltpu.VMEM((2 * bands, TILE), f32),
            pltpu.VMEM((bands, TILE), f32),
            pltpu.VMEM((2 * bands, TILE), f32),
            pltpu.VMEM((8, LANES), f32),
            pltpu.VMEM((n_row - 1, 8, LANES), f32),
            pltpu.VMEM((bands, LANES), f32),
            pltpu.VMEM((n_col - 1, bands, LANES), f32),
            pltpu.SemaphoreType.DMA((2,)),
            pltpu.SemaphoreType.DMA((2,)),
            pltpu.SemaphoreType.DMA,
            pltpu.SemaphoreType.DMA((n_row - 1,)),
            pltpu.SemaphoreType.DMA,
            pltpu.SemaphoreType.DMA((n_col - 1,)),
            pltpu.SemaphoreType.DMA((bands,)),
            pltpu.SemaphoreType.DMA((len(consts),)),
        ],
        compiler_params=pltpu.CompilerParams(
            collective_id=0, has_side_effects=True, vmem_limit_bytes=59 << 20),
        name="chain",
    )(x, *[jnp.asarray(t) for t in consts])

    return pl.pallas_call(
        finish_kernel,
        out_shape=jax.ShapeDtypeStruct(x.shape, f32),
        in_specs=[vmem, vmem],
        out_specs=hbm,
        scratch_shapes=[
            pltpu.VMEM((height, width), f32),
            pltpu.SemaphoreType.DMA((bands,)),
        ],
        compiler_params=pltpu.CompilerParams(vmem_limit_bytes=16 << 20),
        name="finish",
    )(u, offsets)


def solution(mesh):
    n_row, n_col = mesh.shape["row"], mesh.shape["col"]
    return jax.shard_map(
        functools.partial(per_device, n_row, n_col), mesh=mesh,
        in_specs=(P("row", "col"),), out_specs=P("row", "col"), check_vma=False,
    )
```

time: 29 us -> 19.5 us (0.67)
  Pallas kernels: 28.8 us -> 19.3 us
    pallas_call x1, Pallas kernels: 7.36 us -> 2.11 us  [per_device(): pl.pallas_call(finish_kernel, out_shape=jax.ShapeDtypeStruct(x.shape, f32...]
    pallas_call x1, Pallas kernels: 21.5 us -> 17.2 us  [per_device(): pl.pallas_call(functools.partial(chain_kernel, n_row, n_col), out_shape=[...]
where the time goes in v1:
time: 19.5 us; the launch traced here: 19.3 us
  Pallas kernels  19.3 us (99%)
    pallas_call x1, Pallas kernels, per_device(): pl.pallas_call(functools.partial(chain_kernel, n_row, n_col), out_shape=[...  17.2 us
    pallas_call x1, Pallas kernels, per_device(): pl.pallas_call(finish_kernel, out_shape=jax.ShapeDtypeStruct(x.shape, f32...  2.11 us

profile of v1, /device:TPU:0, one launch (start us, length us, event | category | flops | bytes accessed | tf_op | source)
XLA Modules:
  0.0 19.3 jit_solution(13082138604562098381)
XLA Ops:
  0.0 17.2 %chain.1 = (f32[2048,512]{1,0:T(8,128)S(1)}, f32[8,512]{1,0:T(8,128)S(1)}) custom-call(f32[2048,512]{1,0:T(8,128)} %x_hbm.1, f32[256,640]{1,0:T(8,128)} %constant.12.clone.w_hbm, bf16[4,256,128]{2,1,0:T(8,128)(2,1)} %constant.13.clone.left_hbm, bf16[2,512,128]{2,1,0:T(8,128)(2,1)} %constant.14.clone.right_hbm, ...), custom_call_target="tpu_custom_call" | custom-call | tf_op jit(solution)/shard_map/chain/pallas_call | solution.py:394
  17.2 2.1 %finish.1 = f32[2048,512]{1,0:T(8,128)} custom-call(f32[2048,512]{1,0:T(8,128)S(1)} %get-tuple-element.7.u_ref, f32[8,512]{1,0:T(8,128)S(1)} %get-tuple-element.8.off_ref), custom_call_target="tpu_custom_call" | custom-call | tf_op jit(solution)/shard_map/finish/pallas_call | solution.py:432

commit v2 on v1

v2 whole, which is shorter than its diff:
```python
import functools
import math

import jax
import jax.numpy as jnp
import numpy as np
from jax import lax
from jax.experimental import pallas as pl
from jax.experimental.pallas import tpu as pltpu
from jax.sharding import PartitionSpec as P

TILE = 256
FULL_TURN = 2.0 * math.pi
MESH = pl.DeviceIdType.MESH
LANES = 128


def wrap_turns(values):
    return values - jnp.round(values)


def cos32(angle):
    return np.cos(angle.astype(np.float64)).astype(np.float32)


def tables(length):
    f32 = np.float32
    order = np.arange(length, dtype=f32)
    angle = (f32(math.pi) * order)[:, None] * (f32(2) * order + f32(1))[None, :] / f32(2 * length)
    cosine = cos32(angle) * f32(math.sqrt(2.0 / length))
    cosine[0] = cosine[0] * f32(math.sqrt(0.5))
    wave = f32(2) * cos32(f32(math.pi) * order / f32(length))
    eigen = (wave[:, None] + wave[None, :]) - f32(4)
    eigen[0, 0] = -1
    inverse = 1.0 / eigen.astype(np.float64)
    inverse[0, 0] = 0
    c64 = cosine.astype(np.float64)
    weights = []
    for cell in (length - 1, 0):
        green = (c64[:, cell] * inverse[0]) @ c64
        step = green - np.append(green[1:], 0.0)
        step[-1] = 0
        weights.append(step / length)
    return cosine, inverse.astype(f32), np.stack(weights).astype(f32)


def split(values):
    high = values.astype(jnp.bfloat16)
    low = (values - high.astype(jnp.float32)).astype(jnp.bfloat16)
    return high, low


def dot(left, right):
    return jnp.dot(left, right, preferred_element_type=jnp.float32)


def stack3(high, low, axis):
    return jnp.concatenate([high, low, high], axis)


BLOCKS = TILE // LANES


def wide(ref, first, rows):
    return jnp.concatenate([ref[first + l, rows, :] for l in range(BLOCKS)], 1)


def put_wide(ref, first, rows, values):
    for l in range(values.shape[1] // LANES):
        ref[first + l, rows, :] = values[:, l * LANES : (l + 1) * LANES]


def in_blocks(table):
    return np.ascontiguousarray(
        table.reshape(table.shape[0], -1, LANES).transpose(1, 0, 2))


def sandwich(pairs, right, left):
    first, second = pl.ds(0, TILE), pl.ds(TILE, TILE)
    table = [wide(right, 0, first), wide(right, 0, first), wide(right, 0, second)]
    table = jnp.concatenate(table, 0)
    inner = [split(dot(stack3(high, low, 1), table)) for high, low in pairs]
    table = [wide(left, 0, first), wide(left, 0, first), wide(left, BLOCKS, first)]
    table = jnp.concatenate(table, 1)
    return [dot(table, stack3(high, low, 0)) for high, low in inner]


def group_size(bands, most):
    return next(g for g in range(most, 0, -1) if bands % g == 0)


def band_rows(i):
    return pl.ds(pl.multiple_of(i * TILE, TILE), TILE)


def band_copy(src, dst, sem, i):
    rows = band_rows(i)
    view = lambda ref: ref.at[rows, :] if len(ref.shape) == 2 else ref.at[:, rows, :]
    return pltpu.make_async_copy(view(src), view(dst), sem.at[i])


def lane_sum(values):
    return jnp.sum(values, axis=1, keepdims=True)


def running(values):
    n = values.shape[0]
    row = lax.broadcasted_iota(jnp.int32, values.shape, 0)
    total = jnp.zeros_like(values)
    for k in range(n - 1):
        total = total + jnp.where(row > k, values[k : k + 1], 0.0)
    return total


def band_sums(values, bands):
    span = TILE // 8
    row = lax.broadcasted_iota(jnp.int32, (bands, LANES), 0)
    lane = lax.broadcasted_iota(jnp.int32, (bands, LANES), 1)
    per = LANES // span
    sums = jnp.sum(values.reshape(-1, 8, LANES), axis=1)
    picked = jnp.concatenate(
        [jnp.broadcast_to(sums[i // per : i // per + 1], (1, LANES)) for i in range(bands)], 0)
    return lane_sum(jnp.where(lane // span == row % per, picked, 0.0))


LOW = 8
STEP = 16
SPAN = 32


def low_tables(length, bands):
    order = np.arange(length, dtype=np.float64)
    exact = np.cos(np.pi * order[:, None] * (2 * order + 1) / (2 * length)) * math.sqrt(2.0 / length)
    exact[0] *= math.sqrt(0.5)
    wave = 2 * np.cos(np.pi * order / length)
    eigen = wave[:, None] + wave[None, :] - 4
    inverse = tables(length)[1].astype(np.float64)
    change = (eigen * inverse - 1)[:LOW, :LOW]
    change[0, 0] = 0
    means = exact[:LOW].reshape(LOW, length // SPAN, SPAN // 8, 8).mean(2).reshape(LOW, -1)
    full = np.zeros((bands * LOW, LANES), np.float32)
    full[:, :LOW] = np.tile(change, (bands, 1))
    return np.kron(np.eye(bands), means).astype(np.float32), full


def slope_band(x_s, wl_ref, wf_ref, step_ref, net_ref, i, d_s, xb_s, cols_s, sum_x, sum_n, sum_l, sum_f):
    blocks = x_s.shape[0]
    base = pl.multiple_of(i * TILE, TILE) + 8
    shape = (STEP, LANES)
    row = lax.broadcasted_iota(jnp.int32, shape, 0)
    lane8 = lax.broadcasted_iota(jnp.int32, (8, LANES), 1)
    bottom, top = row == STEP - 1, row == 0
    f32, bf16 = jnp.float32, jnp.bfloat16
    none = jnp.zeros(shape, bf16)
    zero = jnp.zeros((8, LANES), f32)
    fold = lambda v: v[0:8] + v[8:16]
    counts = lambda v: jnp.round(v * bf16(1.0 / FULL_TURN))
    groups = range(0, TILE, STEP)
    near = [x_s[l, pl.ds(base, TILE), :].astype(bf16) for l in range(blocks)]
    nets, totals = [], []
    for t in range(blocks // BLOCKS):
        some = near[t * BLOCKS : (t + 2) * BLOCKS]
        n = dot(jnp.concatenate(some, 1), step_ref[0 : len(some) * LANES, :])
        n = counts(n.astype(bf16))
        totals.append(functools.reduce(jnp.add, [n[g : g + STEP] for g in groups]))
        nets.append(dot(n, net_ref[...]).astype(bf16))
    acc_x = [zero] * blocks
    acc_l, acc_f = zero, zero
    first, last = zero, zero
    part = [None] * blocks
    halves = [None] * blocks
    for g in groups:
        x = [x_s[l, pl.ds(base + g, STEP), :] for l in range(blocks)]
        tall, whole = [], []
        for l in range(blocks):
            if g == TILE - STEP:
                below = jnp.where(bottom, x[l], pltpu.roll(x[l], STEP - 1, 0))
            else:
                below = x_s[l, pl.ds(base + g + 1, STEP), :]
            above = x_s[l, pl.ds(base + g - 1, STEP), :]
            mine = near[l][g : g + STEP]
            down = counts(below.astype(bf16) - mine)
            up = counts(mine - above.astype(bf16))
            if g == 0:
                up = jnp.where(top, none, up)
            if l < BLOCKS:
                tall.append(below - x[l])
                whole.append(down)
            net = nets[l // BLOCKS][g : g + STEP, l % BLOCKS * LANES : (l % BLOCKS + 1) * LANES]
            d_s[l, pl.ds(base - 8 + g, STEP), :] = net + (down - up)
            half = fold(x[l])
            if g % SPAN == 0:
                part[l] = half
            else:
                total = part[l] + half
                acc_x[l] = acc_x[l] + total
                if g % (2 * SPAN) == STEP:
                    halves[l] = total
                else:
                    xb_s[l, pl.ds(pl.multiple_of(i * (TILE // 4), 16) + g // (2 * SPAN) * 16, 16), :] = (
                        jnp.concatenate([halves[l], total], 0).astype(bf16))
        slope = functools.reduce(jnp.add, tall) * (1.0 / FULL_TURN)
        slope = slope - functools.reduce(jnp.add, whole).astype(f32)
        acc_l = acc_l + fold(slope * wl_ref[g : g + STEP, :])
        acc_f = acc_f + fold(slope * wf_ref[g : g + STEP, :])
        for j in range(STEP // 8):
            k = g // 8 + j
            cells = slice(8 * j, 8 * j + 8)
            first = jnp.where(lane8 == k, pltpu.roll(x[0][cells], k, 1) if k else x[0][cells], first)
            last = jnp.where(lane8 == k, pltpu.roll(x[-1][cells], k + 1, 1), last)
    here = pl.ds(pl.multiple_of(i * 8, 8), 8)
    cols_s[0, here, :] = first
    cols_s[1, here, :] = last
    sum_x[pl.ds(i, 1), :] = jnp.sum(jnp.concatenate(acc_x, 1), axis=0, keepdims=True)
    sum_n[pl.ds(i, 1), :] = jnp.sum(jnp.concatenate(totals, 1).astype(f32), axis=0, keepdims=True)
    sum_l[pl.ds(i, 1), :] = jnp.sum(acc_l, axis=0, keepdims=True)
    sum_f[pl.ds(i, 1), :] = jnp.sum(acc_f, axis=0, keepdims=True)


def gather_cols(cols_s, side, bands):
    span = TILE // 8
    per = LANES // span
    rows = []
    for g in range(0, bands, per):
        parts = [cols_s[side, (g + j) * 8 : (g + j + 1) * 8, :] for j in range(per)]
        parts = [pltpu.roll(v, j * span, 1) if j else v for j, v in enumerate(parts)]
        rows.append(functools.reduce(jnp.add, parts))
    return jnp.concatenate(rows, 0)


def chain_kernel(
    n_row, n_col, x_hbm, step_hbm, net_hbm, wl_hbm, wf_hbm, w_hbm, left_hbm, right_hbm, left_t_hbm, right_t_hbm, inv_hbm,
    low_hbm, change_hbm, u_ref, off_ref,
    x_s, step_ref, net_ref, wl_ref, wf_ref, w_ref, left, right, left_t, right_t, inv_ref, low_ref, change_ref,
    d_s, xb_s, cols_s, corr_s, sum_x, sum_n, sum_l, sum_f,
    col_out, col_in, down_out, down_in, row_out, row_in,
    edge_send, edge_recv, down_send, down_recv, row_send, row_recv,
    x_sem, table_sem,
):
    r, c = lax.axis_index("row"), lax.axis_index("col")
    blocks, height = x_s.shape[0], x_s.shape[1] - 16
    bands, tiles = height // TILE, blocks // BLOCKS

    def x_copy(i, l):
        return pltpu.make_async_copy(
            x_hbm.at[band_rows(i), l * LANES : (l + 1) * LANES], x_s.at[l, pl.ds(pl.multiple_of(i * TILE, TILE) + 8, TILE), :],
            x_sem.at[i, l])

    def fetch(i, carry):
        for l in range(blocks):
            x_copy(i, l).start()
        return carry

    def arrive(i):
        for l in range(blocks):
            x_copy(i, l).wait()

    copies = [(step_hbm, step_ref), (net_hbm, net_ref), (wl_hbm, wl_ref), (wf_hbm, wf_ref), (w_hbm, w_ref), (right_hbm, right), (left_hbm, left),
              (inv_hbm, inv_ref), (low_hbm, low_ref), (change_hbm, change_ref),
              (right_t_hbm, right_t), (left_t_hbm, left_t)]
    copies = [pltpu.make_async_copy(a, b, table_sem.at[k]) for k, (a, b) in enumerate(copies)]
    fetch(0, 0)
    for copy in copies[:4]:
        copy.start()
    lax.fori_loop(1, bands, fetch, 0)
    for copy in copies[4:]:
        copy.start()

    barrier = pltpu.get_barrier_semaphore()

    def greet(row, col):
        pl.semaphore_signal(barrier, inc=1, device_id=(row, col), device_id_type=MESH)

    def greet_above(k, carry):
        greet(k, 0)
        return carry

    def greet_left(k, carry):
        greet(r, k)
        return carry

    is_first = c == 0
    has_right = c < n_col - 1
    lax.fori_loop(0, r, greet_above, 0)
    lax.fori_loop(0, c, greet_left, 0)
    pl.when(has_right)(lambda: greet(r, c + 1))

    pair = group_size(bands, 2)

    def slopes(j, carry):
        for k in range(pair):
            arrive(j * pair + k)
        for k in range(pair):
            slope_band(x_s, wl_ref, wf_ref, step_ref, net_ref, j * pair + k,
                       d_s, xb_s, cols_s, sum_x, sum_n, sum_l, sum_f)
        return carry

    for copy in copies[:4]:
        copy.wait()
    lax.fori_loop(0, bands // pair, slopes, 0)
    col_out[...] = gather_cols(cols_s, 0, bands)
    edge_col = pltpu.make_async_remote_copy(
        src_ref=col_out, dst_ref=col_in, send_sem=edge_send, recv_sem=edge_recv,
        device_id=(r, jnp.maximum(c - 1, 0)), device_id_type=MESH)

    @pl.when(jnp.logical_not(is_first))
    def _():
        pl.semaphore_wait(barrier, n_col - c)
        edge_col.start()

    scale = FULL_TURN / TILE
    down_last = lane_sum(sum_l[...])
    down_first = lane_sum(sum_f[...])
    border = jnp.zeros((bands - 1, LANES), jnp.float32)
    for l in range(BLOCKS):
        ends = [x_s[l, i * TILE + 7 : i * TILE + 9, :] for i in range(1, bands)]
        ends = [v[1:2] - v[0:1] for v in ends]
        border = border + wrap_turns(jnp.concatenate(ends, 0) * (1.0 / FULL_TURN))
    border = lane_sum(border) * scale
    zero = jnp.zeros((1, 1), jnp.float32)
    jump = down_last + jnp.concatenate([border - down_first[1:bands], zero], 0)
    jump_total = jnp.sum(jump, axis=0, keepdims=True) - down_first[0:1]
    starts = running(jump)
    starts = starts - jnp.where(r > 0, down_first[0:1], 0.0)
    lane = lax.broadcasted_iota(jnp.int32, (1, LANES), 1)
    tops = [x_s[l, 8:9, :] for l in range(BLOCKS)]
    scalars = jnp.where(lane == 0, jump_total, jnp.where(lane == 1, down_first[0:1], 0.0))
    down_out[...] = jnp.concatenate(
        tops + [x_s[l, height + 7 : height + 8, :] for l in range(BLOCKS)] + [scalars], 0)

    down_copy = lambda row, col: pltpu.make_async_remote_copy(
        src_ref=down_out, dst_ref=down_in.at[r], send_sem=down_send, recv_sem=down_recv.at[r],
        device_id=(row, col), device_id_type=MESH)
    row_copy = lambda k: pltpu.make_async_remote_copy(
        src_ref=row_out, dst_ref=row_in.at[c], send_sem=row_send, recv_sem=row_recv.at[c],
        device_id=(r, k), device_id_type=MESH)
    for copy in copies[4:]:
        copy.wait()
    first, second = pl.ds(0, TILE), pl.ds(TILE, TILE)
    for t in range(tiles):
        low = jnp.concatenate([xb_s[t * BLOCKS + k] for k in range(BLOCKS)], 1)
        low = dot(low, right[0, first, :]).astype(jnp.bfloat16)
        corr_s[t] = dot(low_ref[...], low) * change_ref[...]

    def solve(some):
        places = [(i, t) for i in some for t in range(tiles)]
        table = jnp.concatenate([wide(right, 0, first), wide(right, 0, second)], 0)
        data = [wide(d_s, t * BLOCKS, band_rows(i)) for i, t in places]
        inner = [split(dot(jnp.concatenate([d, d], 1), table)) for d in data]
        table = [wide(left, 0, first), wide(left, 0, first), wide(left, BLOCKS, first)]
        table = jnp.concatenate(table, 1)
        pairs = []
        for (i, t), (high, low) in zip(places, inner):
            scaled = dot(table, stack3(high, low, 0)) * inv_ref[...]
            corner = scaled[0:LOW, 0:LANES] + corr_s[t, i * LOW : (i + 1) * LOW, :]
            scaled = jnp.concatenate(
                [jnp.concatenate([corner, scaled[0:LOW, LANES:]], 1), scaled[LOW:]], 0)
            pairs.append(split(scaled))
        for (i, t), solved in zip(places, sandwich(pairs, right_t, left_t)):
            u_ref[band_rows(i), t * TILE : (t + 1) * TILE] = (
                solved + wide(x_s, t * BLOCKS, pl.ds(i * TILE + 8, TILE)))

    solve(range(0, 2))

    def each_below(act):
        def per_row(k, carry):
            def per_col(j, carry):
                act(down_copy(n_row - 1 - k, n_col - 1 - j))
                return carry
            return lax.fori_loop(0, n_col, per_col, carry)
        lax.fori_loop(0, jnp.where(is_first, n_row - 1 - r, 0), per_row, 0)

    @pl.when(is_first)
    def _():
        pl.semaphore_wait(barrier, (n_row - 1 - r) * n_col + n_col - 1)

    each_below(lambda copy: copy.start())

    last_col = gather_cols(cols_s, 1, bands)
    sums = sum_x[...]
    mean = [lane_sum(sums[:, t * TILE : (t + 1) * TILE]) * (1.0 / TILE / TILE) for t in range(tiles)]
    sums = (pltpu.roll(sums, blocks * LANES - 1, 1) - sums) * (1.0 / FULL_TURN) - sum_n[...]
    last_w, first_w = w_ref[0:1, 0:TILE], w_ref[0:1, TILE : 2 * TILE]
    lasts = [lane_sum(sums[:, t * TILE : (t + 1) * TILE] * last_w) for t in range(tiles)]
    firsts = [lane_sum(sums[:, t * TILE : (t + 1) * TILE] * first_w) for t in range(tiles)]
    along = [jnp.zeros((bands, 1), jnp.float32)]
    for t in range(tiles - 1):
        end = (t + 1) * TILE
        along.append(along[-1] + lasts[t] + sums[:, end - 1 : end] * scale - firsts[t + 1])

    pl.when(has_right)(lambda: edge_col.wait_recv())
    edge = wrap_turns((col_in[...] - last_col) * (1.0 / FULL_TURN))
    row_total = along[-1] + lasts[-1] + band_sums(edge, bands) * scale - firsts[0]
    lane = lax.broadcasted_iota(jnp.int32, (bands, LANES), 1)
    row_out[0:bands, :] = jnp.where(
        lane == 0, row_total, jnp.where(lane == 1, starts + firsts[0], 0.0))
    row_out[bands : bands + BLOCKS, :] = jnp.concatenate(tops, 0)

    def send_row(k, carry):
        row_copy(k).start()
        return carry

    lax.fori_loop(c + 1, n_col, send_row, 0)

    for k in range(2, bands, 3):
        solve(range(k, min(k + 3, bands)))

    pl.when(jnp.logical_not(is_first))(lambda: edge_col.wait_send())

    each_below(lambda copy: copy.wait_send())

    def sent_row(k, carry):
        row_copy(k).wait_send()
        return carry

    lax.fori_loop(c + 1, n_col, sent_row, 0)

    offset = jnp.where(is_first, starts, -firsts[0])
    for k in range(n_col - 1):
        pl.when(k < c)(lambda: pltpu.make_async_remote_copy(
            src_ref=row_out, dst_ref=row_in.at[k], send_sem=row_send, recv_sem=row_recv.at[k],
            device_id=(r, c), device_id_type=MESH).wait_recv())
        offset = offset + jnp.where(k < c, row_in[k, 0:bands, 0:1], 0.0)
    offset = offset + jnp.where(c > 0, row_in[0, 0:bands, 1:2], 0.0)

    for k in range(n_row - 1):
        pl.when(k < r)(lambda: pltpu.make_async_remote_copy(
            src_ref=down_out, dst_ref=down_in.at[k], send_sem=down_send, recv_sem=down_recv.at[k],
            device_id=(r, c), device_id_type=MESH).wait_recv())
    edge = jnp.zeros((n_row - 1, LANES), jnp.float32)
    number = lax.broadcasted_iota(jnp.int32, (n_row - 1, LANES), 0)
    for l in range(BLOCKS):
        own = jnp.where(is_first, tops[l], row_in[0, bands + l : bands + l + 1, :])
        upper = jnp.concatenate([down_in[k, BLOCKS + l : BLOCKS + l + 1, :] for k in range(n_row - 1)], 0)
        lower = jnp.concatenate([down_in[k, l : l + 1, :] for k in range(1, n_row - 1)] + [own], 0)
        lower = jnp.where(number == r - 1, own, lower)
        edge = edge + wrap_turns((lower - upper) * (1.0 / FULL_TURN))
    single = jnp.concatenate([down_in[k, 2 * BLOCKS : 2 * BLOCKS + 1, :] for k in range(n_row - 1)], 0)
    lane = lax.broadcasted_iota(jnp.int32, (n_row - 1, LANES), 1)
    pick = jnp.where(lane == 0, single, 0.0) + jnp.where((lane == 1) & (number == 0), single, 0.0)
    above = jnp.where(number < r, edge * scale + pick, 0.0)
    above = lane_sum(jnp.sum(above, axis=0, keepdims=True))
    offset = offset + above
    for t in range(tiles):
        off_ref[:, t * TILE : (t + 1) * TILE] = jnp.broadcast_to(
            offset + along[t] - mean[t], (bands, TILE))


def finish_kernel(u_ref, off_ref, out_hbm, out_s, out_sem):
    height, width = out_s.shape
    bands = height // TILE
    for i in range(bands):
        rows = band_rows(i)
        out_s[rows, :] = u_ref[rows, :] + off_ref[i : i + 1, :]
        band_copy(out_s, out_hbm, out_sem, i).start()
    for i in range(bands):
        band_copy(out_s, out_hbm, out_sem, i).wait()


def per_device(n_row, n_col, x):
    height, width = x.shape
    bands = height // TILE
    blocks = width // LANES
    tiles = width // TILE
    cosine, inverse, weights = tables(TILE)
    high = cosine.astype(jnp.bfloat16)
    low = (cosine - high.astype(np.float32)).astype(jnp.bfloat16)
    beside = in_blocks(np.concatenate([high, low], 1))
    over = in_blocks(np.concatenate([high, low], 0))
    beside_t = in_blocks(np.concatenate([high.T, low.T], 1))
    over_t = in_blocks(np.concatenate([high.T, low.T], 0))
    weights = weights * np.float32(FULL_TURN)
    w = np.tile(weights.reshape(1, -1), (8, 1))
    wl = np.ascontiguousarray(np.broadcast_to(weights[0][:, None], (TILE, LANES)))
    wf = np.ascontiguousarray(np.broadcast_to(weights[1][:, None], (TILE, LANES)))
    means, change = low_tables(TILE, bands)
    eye = np.eye(2 * TILE, TILE, dtype=np.float32)
    step = np.eye(2 * TILE, TILE, -1, dtype=np.float32) - eye
    net = np.eye(TILE, dtype=np.float32) - np.eye(TILE, k=1, dtype=np.float32)
    net[TILE - 1] = 0

    vmem = pl.BlockSpec(memory_space=pltpu.VMEM)
    hbm = pl.BlockSpec(memory_space=pltpu.HBM)
    f32, bf16 = jnp.float32, jnp.bfloat16
    consts = [step.astype(bf16), net.astype(bf16), wl, wf, w, beside, over_t, beside_t, over, inverse * np.float32(-FULL_TURN),
              means.astype(bf16), change]
    u, offsets = pl.pallas_call(
        functools.partial(chain_kernel, n_row, n_col),
        out_shape=[pltpu.VMEM(x.shape, f32), pltpu.VMEM((bands, width), f32)],
        in_specs=[hbm] * (1 + len(consts)),
        out_specs=[vmem, vmem],
        scratch_shapes=[pltpu.VMEM((blocks, height + 16, LANES), f32)]
        + [pltpu.VMEM(t.shape, t.dtype) for t in consts]
        + [
            pltpu.VMEM((blocks, height, LANES), bf16),
            pltpu.VMEM((blocks, height // 4, LANES), bf16),
            pltpu.VMEM((2, bands * 8, LANES), f32),
            pltpu.VMEM((tiles, bands * LOW, LANES), f32),
            pltpu.VMEM((bands, width), f32),
            pltpu.VMEM((bands, width), f32),
            pltpu.VMEM((bands, LANES), f32),
            pltpu.VMEM((bands, LANES), f32),
            pltpu.VMEM((height // LANES, LANES), f32),
            pltpu.VMEM((height // LANES, LANES), f32),
            pltpu.VMEM((2 * BLOCKS + 1, LANES), f32),
            pltpu.VMEM((n_row - 1, 2 * BLOCKS + 1, LANES), f32),
            pltpu.VMEM((bands + BLOCKS, LANES), f32),
            pltpu.VMEM((n_col - 1, bands + BLOCKS, LANES), f32),
            pltpu.SemaphoreType.DMA,
            pltpu.SemaphoreType.DMA,
            pltpu.SemaphoreType.DMA,
            pltpu.SemaphoreType.DMA((n_row - 1,)),
            pltpu.SemaphoreType.DMA,
            pltpu.SemaphoreType.DMA((n_col - 1,)),
            pltpu.SemaphoreType.DMA((bands, blocks)),
            pltpu.SemaphoreType.DMA((len(consts),)),
        ],
        compiler_params=pltpu.CompilerParams(
            collective_id=0, has_side_effects=True, vmem_limit_bytes=59 << 20),
        name="chain",
    )(x, *[jnp.asarray(t) for t in consts])

    return pl.pallas_call(
        finish_kernel,
        out_shape=jax.ShapeDtypeStruct(x.shape, f32),
        in_specs=[vmem, vmem],
        out_specs=hbm,
        scratch_shapes=[
            pltpu.VMEM((height, width), f32),
            pltpu.SemaphoreType.DMA((bands,)),
        ],
        compiler_params=pltpu.CompilerParams(vmem_limit_bytes=16 << 20),
        name="finish",
    )(u, offsets)


def solution(mesh):
    n_row, n_col = mesh.shape["row"], mesh.shape["col"]
    return jax.shard_map(
        functools.partial(per_device, n_row, n_col), mesh=mesh,
        in_specs=(P("row", "col"),), out_specs=P("row", "col"), check_vma=False,
    )
```

time: 19.5 us -> 18 us (0.923)
  Pallas kernels: 19.3 us -> 17.8 us
    pallas_call x1, Pallas kernels: 17.2 us -> 15.7 us  [per_device(): pl.pallas_call(functools.partial(chain_kernel, n_row, n_col), out_shape=[...]
where the time goes in v2:
time: 18 us; the launch traced here: 17.9 us
  Pallas kernels  17.8 us (99%)
    pallas_call x1, Pallas kernels, per_device(): pl.pallas_call(functools.partial(chain_kernel, n_row, n_col), out_shape=[...  15.7 us
    pallas_call x1, Pallas kernels, per_device(): pl.pallas_call(finish_kernel, out_shape=jax.ShapeDtypeStruct(x.shape, f32...  2.11 us

profile of v2, /device:TPU:0, one launch (start us, length us, event | category | flops | bytes accessed | tf_op | source)
XLA Modules:
  0.0 17.9 jit_solution(7324446854513815481)
XLA Ops:
  0.0 15.7 %chain.1 = (f32[2048,512]{1,0:T(8,128)S(1)}, f32[8,512]{1,0:T(8,128)S(1)}) custom-call(f32[2048,512]{1,0:T(8,128)} %x_hbm.1, bf16[512,256]{1,0:T(8,128)(2,1)} %constant.24.clone.step_hbm, bf16[256,256]{1,0:T(8,128)(2,1)} %constant.25.clone.net_hbm, f32[256,128]{1,0:T(8,128)} %constant.26.clone.wl_hbm, f32[256,128]{1,0:T(8,128)} %constant.27.clone.wf_hbm, ...), custom_call_target="tpu_custom_call" | custom-call | tf_op jit(solution)/shard_map/chain/pallas_call | solution.py:487
  15.7 2.1 %finish.1 = f32[2048,512]{1,0:T(8,128)} custom-call(f32[2048,512]{1,0:T(8,128)S(1)} %get-tuple-element.7.u_ref, f32[8,512]{1,0:T(8,128)S(1)} %get-tuple-element.8.off_ref), custom_call_target="tpu_custom_call" | custom-call | tf_op jit(solution)/shard_map/finish/pallas_call | solution.py:523

commit v3 on v2

--- a/solution.py
+++ b/solution.py
@@ -370,11 +370,15 @@
             return lax.fori_loop(0, n_col, per_col, carry)
         lax.fori_loop(0, jnp.where(is_first, n_row - 1 - r, 0), per_row, 0)
 
-    @pl.when(is_first)
-    def _():
-        pl.semaphore_wait(barrier, (n_row - 1 - r) * n_col + n_col - 1)
-
-    each_below(lambda copy: copy.start())
+    def send_down(when):
+        @pl.when(jnp.logical_and(is_first, when))
+        def _():
+            pl.semaphore_wait(barrier, (n_row - 1 - r) * n_col + n_col - 1)
+            each_below(lambda copy: copy.start())
+
+    send_down(r > 0)
+    solve(range(2, 4))
+    send_down(r == 0)
 
     last_col = gather_cols(cols_s, 1, bands)
     sums = sum_x[...]
@@ -402,8 +406,8 @@
 
     lax.fori_loop(c + 1, n_col, send_row, 0)
 
-    for k in range(2, bands, 3):
-        solve(range(k, min(k + 3, bands)))
+    for k in range(4, bands, 4):
+        solve(range(k, min(k + 4, bands)))
 
     pl.when(jnp.logical_not(is_first))(lambda: edge_col.wait_send())
 

time: 18 us -> 16.5 us (0.917)
  Pallas kernels: 17.8 us -> 16.3 us
    pallas_call x1, Pallas kernels: 15.7 us -> 14.2 us  [per_device(): pl.pallas_call(functools.partial(chain_kernel, n_row, n_col), out_shape=[...]
where the time goes in v3:
time: 16.5 us; the launch traced here: 16.4 us
  Pallas kernels  16.3 us (99%)
    pallas_call x1, Pallas kernels, per_device(): pl.pallas_call(functools.partial(chain_kernel, n_row, n_col), out_shape=[...  14.2 us
    pallas_call x1, Pallas kernels, per_device(): pl.pallas_call(finish_kernel, out_shape=jax.ShapeDtypeStruct(x.shape, f32...  2.11 us

profile of v3, /device:TPU:0, one launch (start us, length us, event | category | flops | bytes accessed | tf_op | source)
XLA Modules:
  0.0 16.4 jit_solution(4981382626328429649)
XLA Ops:
  0.0 14.2 %chain.1 = (f32[2048,512]{1,0:T(8,128)S(1)}, f32[8,512]{1,0:T(8,128)S(1)}) custom-call(f32[2048,512]{1,0:T(8,128)} %x_hbm.1, bf16[512,256]{1,0:T(8,128)(2,1)} %constant.24.clone.step_hbm, bf16[256,256]{1,0:T(8,128)(2,1)} %constant.25.clone.net_hbm, f32[256,128]{1,0:T(8,128)} %constant.26.clone.wl_hbm, f32[256,128]{1,0:T(8,128)} %constant.27.clone.wf_hbm, ...), custom_call_target="tpu_custom_call" | custom-call | tf_op jit(solution)/shard_map/chain/pallas_call | solution.py:491
  14.2 2.1 %finish.1 = f32[2048,512]{1,0:T(8,128)} custom-call(f32[2048,512]{1,0:T(8,128)S(1)} %get-tuple-element.7.u_ref, f32[8,512]{1,0:T(8,128)S(1)} %get-tuple-element.8.off_ref), custom_call_target="tpu_custom_call" | custom-call | tf_op jit(solution)/shard_map/finish/pallas_call | solution.py:527

commit v4 on v3

--- a/solution.py
+++ b/solution.py
@@ -156,58 +156,62 @@
     fold = lambda v: v[0:8] + v[8:16]
     counts = lambda v: jnp.round(v * bf16(1.0 / FULL_TURN))
     groups = range(0, TILE, STEP)
-    near = [x_s[l, pl.ds(base, TILE), :].astype(bf16) for l in range(blocks)]
-    nets, totals = [], []
-    for t in range(blocks // BLOCKS):
-        some = near[t * BLOCKS : (t + 2) * BLOCKS]
-        n = dot(jnp.concatenate(some, 1), step_ref[0 : len(some) * LANES, :])
-        n = counts(n.astype(bf16))
-        totals.append(functools.reduce(jnp.add, [n[g : g + STEP] for g in groups]))
-        nets.append(dot(n, net_ref[...]).astype(bf16))
+    near_of = lambda l, g, size: x_s[l, pl.ds(base + g, size), :].astype(bf16)
+    totals = []
     acc_x = [zero] * blocks
     acc_l, acc_f = zero, zero
     first, last = zero, zero
-    part = [None] * blocks
-    halves = [None] * blocks
-    for g in groups:
-        x = [x_s[l, pl.ds(base + g, STEP), :] for l in range(blocks)]
-        tall, whole = [], []
-        for l in range(blocks):
-            if g == TILE - STEP:
-                below = jnp.where(bottom, x[l], pltpu.roll(x[l], STEP - 1, 0))
-            else:
-                below = x_s[l, pl.ds(base + g + 1, STEP), :]
-            above = x_s[l, pl.ds(base + g - 1, STEP), :]
-            mine = near[l][g : g + STEP]
-            down = counts(below.astype(bf16) - mine)
-            up = counts(mine - above.astype(bf16))
-            if g == 0:
-                up = jnp.where(top, none, up)
-            if l < BLOCKS:
-                tall.append(below - x[l])
-                whole.append(down)
-            net = nets[l // BLOCKS][g : g + STEP, l % BLOCKS * LANES : (l % BLOCKS + 1) * LANES]
-            d_s[l, pl.ds(base - 8 + g, STEP), :] = net + (down - up)
-            half = fold(x[l])
-            if g % SPAN == 0:
-                part[l] = half
-            else:
-                total = part[l] + half
-                acc_x[l] = acc_x[l] + total
-                if g % (2 * SPAN) == STEP:
-                    halves[l] = total
+    for t in range(blocks // BLOCKS):
+        own = range(t * BLOCKS, (t + 1) * BLOCKS)
+        some = range(t * BLOCKS, min((t + 2) * BLOCKS, blocks))
+        n = dot(jnp.concatenate([near_of(l, 0, TILE) for l in some], 1),
+                step_ref[0 : len(some) * LANES, :])
+        n = counts(n.astype(bf16))
+        totals.append(functools.reduce(jnp.add, [n[g : g + STEP] for g in groups]))
+        nets = dot(n, net_ref[...]).astype(bf16)
+        part, halves = {}, {}
+        for g in groups:
+            tall, whole = [], []
+            for l in own:
+                x = x_s[l, pl.ds(base + g, STEP), :]
+                mine = x.astype(bf16)
+                if g == TILE - STEP:
+                    below = jnp.where(bottom, x, pltpu.roll(x, STEP - 1, 0))
                 else:
-                    xb_s[l, pl.ds(pl.multiple_of(i * (TILE // 4), 16) + g // (2 * SPAN) * 16, 16), :] = (
-                        jnp.concatenate([halves[l], total], 0).astype(bf16))
-        slope = functools.reduce(jnp.add, tall) * (1.0 / FULL_TURN)
-        slope = slope - functools.reduce(jnp.add, whole).astype(f32)
-        acc_l = acc_l + fold(slope * wl_ref[g : g + STEP, :])
-        acc_f = acc_f + fold(slope * wf_ref[g : g + STEP, :])
-        for j in range(STEP // 8):
-            k = g // 8 + j
-            cells = slice(8 * j, 8 * j + 8)
-            first = jnp.where(lane8 == k, pltpu.roll(x[0][cells], k, 1) if k else x[0][cells], first)
-            last = jnp.where(lane8 == k, pltpu.roll(x[-1][cells], k + 1, 1), last)
+                    below = x_s[l, pl.ds(base + g + 1, STEP), :]
+                above = x_s[l, pl.ds(base + g - 1, STEP), :]
+                down = counts(below.astype(bf16) - mine)
+                up = counts(mine - above.astype(bf16))
+                if g == 0:
+                    up = jnp.where(top, none, up)
+                if t == 0:
+                    tall.append(below - x)
+                    whole.append(down)
+                net = nets[g : g + STEP, l % BLOCKS * LANES : (l % BLOCKS + 1) * LANES]
+                d_s[l, pl.ds(base - 8 + g, STEP), :] = net + (down - up)
+                half = fold(x)
+                if g % SPAN == 0:
+                    part[l] = half
+                else:
+                    total = part[l] + half
+                    acc_x[l] = acc_x[l] + total
+                    if g % (2 * SPAN) == STEP:
+                        halves[l] = total
+                    else:
+                        xb_s[l, pl.ds(pl.multiple_of(i * (TILE // 4), 16) + g // (2 * SPAN) * 16, 16), :] = (
+                            jnp.concatenate([halves[l], total], 0).astype(bf16))
+                for j in range(STEP // 8):
+                    k = g // 8 + j
+                    cells = x[8 * j : 8 * j + 8]
+                    if l == 0:
+                        first = jnp.where(lane8 == k, pltpu.roll(cells, k, 1) if k else cells, first)
+                    if l == blocks - 1:
+                        last = jnp.where(lane8 == k, pltpu.roll(cells, k + 1, 1), last)
+            if t == 0:
+                slope = functools.reduce(jnp.add, tall) * (1.0 / FULL_TURN)
+                slope = slope - functools.reduce(jnp.add, whole).astype(f32)
+                acc_l = acc_l + fold(slope * wl_ref[g : g + STEP, :])
+                acc_f = acc_f + fold(slope * wf_ref[g : g + STEP, :])
     here = pl.ds(pl.multiple_of(i * 8, 8), 8)
     cols_s[0, here, :] = first
     cols_s[1, here, :] = last
@@ -285,7 +289,7 @@
     lax.fori_loop(0, c, greet_left, 0)
     pl.when(has_right)(lambda: greet(r, c + 1))
 
-    pair = group_size(bands, 2)
+    pair = group_size(bands, 4)
 
     def slopes(j, carry):
         for k in range(pair):
@@ -411,7 +415,14 @@
 
     pl.when(jnp.logical_not(is_first))(lambda: edge_col.wait_send())
 
-    each_below(lambda copy: copy.wait_send())
+    def sent_below(k, carry):
+        some = down_in.at[0:n_col]
+        pltpu.make_async_remote_copy(
+            src_ref=some, dst_ref=some, send_sem=down_send, recv_sem=down_recv.at[0],
+            device_id=(r, c), device_id_type=MESH).wait_send()
+        return carry
+
+    lax.fori_loop(0, jnp.where(is_first, n_row - 1 - r, 0), sent_below, 0)
 
     def sent_row(k, carry):
         row_copy(k).wait_send()

time: 16.5 us -> 16.3 us (0.988)
    pallas_call x1, Pallas kernels: 14.2 us -> 14.1 us  [per_device(): pl.pallas_call(functools.partial(chain_kernel, n_row, n_col), out_shape=[...]
where the time goes in v4:
time: 16.3 us; the launch traced here: 16.2 us
  Pallas kernels  16.2 us (99%)
    pallas_call x1, Pallas kernels, per_device(): pl.pallas_call(functools.partial(chain_kernel, n_row, n_col), out_shape=[...  14.1 us
    pallas_call x1, Pallas kernels, per_device(): pl.pallas_call(finish_kernel, out_shape=jax.ShapeDtypeStruct(x.shape, f32...  2.11 us

profile of v4, /device:TPU:0, one launch (start us, length us, event | category | flops | bytes accessed | tf_op | source)
XLA Modules:
  0.0 16.2 jit_solution(2569997535642521166)
XLA Ops:
  0.0 14.1 %chain.1 = (f32[2048,512]{1,0:T(8,128)S(1)}, f32[8,512]{1,0:T(8,128)S(1)}) custom-call(f32[2048,512]{1,0:T(8,128)} %x_hbm.1, bf16[512,256]{1,0:T(8,128)(2,1)} %constant.24.clone.step_hbm, bf16[256,256]{1,0:T(8,128)(2,1)} %constant.25.clone.net_hbm, f32[256,128]{1,0:T(8,128)} %constant.26.clone.wl_hbm, f32[256,128]{1,0:T(8,128)} %constant.27.clone.wf_hbm, ...), custom_call_target="tpu_custom_call" | custom-call | tf_op jit(solution)/shard_map/chain/pallas_call | solution.py:502
  14.1 2.1 %finish.1 = f32[2048,512]{1,0:T(8,128)} custom-call(f32[2048,512]{1,0:T(8,128)S(1)} %get-tuple-element.7.u_ref, f32[8,512]{1,0:T(8,128)S(1)} %get-tuple-element.8.off_ref), custom_call_target="tpu_custom_call" | custom-call | tf_op jit(solution)/shard_map/finish/pallas_call | solution.py:538
